TPU v7x, 32 devices: a whole 2x2x4 slice. The times are simulated.
32 devices in a mesh: win: 2 (over core), grp: 16 (over z, y, x).
Axes of the slice: x: 2, y: 2, z: 4, core: 2. Of those that a mesh axis runs over, the one named last changes fastest.
Arguments:
- atom_table: float32 [4, 6, 24576], P('win', None, 'grp'), as said below
- row_blocks: int32 [4, 1024], P('win', 'grp'), may hold values from 0 to 191, as said below
- col_blocks: int32 [4, 1024], P('win', 'grp'), may hold values from 0 to 191, as said below
- lambdas: float32 [4], replicated, may hold values from 0 to 1, as said below
- inverse_temp: float32 [1], replicated, may hold values from 20 to 80
- parity: int32 [1], replicated, may hold values from 0 to 1073741823
- thresholds: int32 [4], replicated, may hold values from 0 to 1073741823
Outputs:
- energies: float32 [4, 3], P('win')
- margins: float32 [4], P('win')
- profile: float32 [4], P('win')
Inputs may be any that keep to these rules, and one draw needn't show every extreme that they name: `row_blocks`: the first block of each pair listed on index g of grp lies in that index's share of atoms: blocks g * 12 to (g + 1) * 12 - 1. `col_blocks`: the list of one index of grp names blocks of any one index of grp (itself included) at most 5 times; in each window some index of grp has exactly 5 of its blocks named in every list of that window. `lambdas`: strictly increasing. `atom_table`: field 4 lies in 0.7 to 1.4 and field 5 in 0.6 to 1.4.
All inputs are finite; a program needn't handle non-finite values.
Results may differ from a plain program's by a relative error of at most 0.0003.
Values sent between devices are 32-bit elements; how exact they have to be, the bound alone decides.
No kernel may reach another device: no remote copies, remote signals or barrier semaphores. Data moves between devices by JAX's collectives and lax.ppermute only.
A program may use at most 64 MiB of HBM per device.

v0:
```python
import jax
import jax.numpy as jnp
from jax import lax
from jax.sharding import PartitionSpec as P

TILE = 128
tiles_per_step = 16


def from_behind(shard, axis, by):
    peers = lax.axis_size(axis)
    pairs = [(i, i + by) for i in range(peers) if 0 <= i + by < peers]
    return lax.ppermute(shard, axis, pairs)


def entering(part, axis, combine, identity):
    place = lax.axis_index(axis)
    gathered = lax.all_gather(part, axis)
    state = jnp.zeros_like(part) + jnp.asarray(identity, part.dtype)

    def one(step, state):
        return combine(state, lax.dynamic_index_in_dim(gathered, step, 0, False))

    return lax.fori_loop(0, place, one, state)


def pair_energy(row_data, col_data, same_block, lambda_set):
    delta_x = row_data[0][:, :, None] - col_data[0][:, None, :]
    delta_y = row_data[1][:, :, None] - col_data[1][:, None, :]
    delta_z = row_data[2][:, :, None] - col_data[2][:, None, :]
    distance = delta_x * delta_x + delta_y * delta_y + delta_z * delta_z
    charge_pair = row_data[3][:, :, None] * col_data[3][:, None, :]
    well_depth = 4.0 * row_data[4][:, :, None] * col_data[4][:, None, :]
    size_pair = row_data[5][:, :, None] * col_data[5][:, None, :]
    scaled = distance / size_pair
    scaled_cube = scaled * scaled * scaled
    width_tile = distance.shape[-1]
    diagonal = (
        lax.broadcasted_iota(jnp.int32, (width_tile, width_tile), 0)
        == lax.broadcasted_iota(jnp.int32, (width_tile, width_tile), 1)
    ).astype(jnp.float32)
    keep_mask = 1.0 - same_block[:, None, None] * diagonal[None]
    totals = []
    for number in range(3):
        lam_now = lambda_set[number]
        softened = 1.0 - 0.5 * lam_now + scaled_cube
        inverse = 1.0 / softened
        dispersion = well_depth * (inverse * inverse - inverse)
        coulomb = charge_pair * lax.rsqrt(distance + 2.0 - lam_now)
        totals.append(lam_now * jnp.sum(keep_mask * (dispersion + coulomb)))
    return jnp.stack(totals)


def evaluate(row_all, col_all, same_all, lambda_set):
    count = same_all.shape[0] // tiles_per_step

    def advance(number, total):
        start = number * tiles_per_step
        row_part = lax.dynamic_slice_in_dim(row_all, start, tiles_per_step, 1)
        col_part = lax.dynamic_slice_in_dim(col_all, start, tiles_per_step, 1)
        same_part = lax.dynamic_slice_in_dim(same_all, start, tiles_per_step, 0)
        return total + pair_energy(row_part, col_part, same_part, lambda_set)

    return lax.fori_loop(0, count, advance, jnp.zeros((3,), jnp.float32))


def add_terms(earlier, later):
    return earlier + later


def take_blocks(source, indices):
    return jnp.take(source, indices, axis=1)


def per_device(atom_table, row_blocks, col_blocks, lambdas, inverse_temp, parity, thresholds):
    windows = lax.axis_size("win") * atom_table.shape[0]
    groups = lax.axis_size("grp")
    window_run = atom_table.shape[0]
    member = lax.axis_index("grp")
    first_window = lax.axis_index("win") * window_run
    fields = atom_table.shape[1]
    blocks_own = atom_table.reshape(window_run, fields, -1, TILE)
    own_count = blocks_own.shape[2]
    listed = row_blocks.shape[1]
    row_data = jax.vmap(take_blocks)(blocks_own, row_blocks - member * own_count)
    slot_count = max(2, 5 * listed // (4 * groups))
    peers = jnp.arange(groups, dtype=jnp.int32)
    slot_ids = jnp.arange(slot_count, dtype=jnp.int32)

    def plan(col_ids):
        owner_ids = col_ids // own_count
        within_ids = col_ids - owner_ids * own_count
        owner_hot = (owner_ids[:, None] == peers[None, :]).astype(jnp.int32)
        earlier_hot = jnp.cumsum(owner_hot, axis=0) - owner_hot
        order_rank = jnp.sum(earlier_hot * owner_hot, axis=1)
        matched = owner_hot[:, :, None] * (
            order_rank[:, None, None] == slot_ids[None, None, :]
        ).astype(jnp.int32)
        requests = jnp.sum(matched * (within_ids + 1)[:, None, None], axis=0) - 1
        return (owner_ids * slot_count + order_rank, requests)

    positions, requests = jax.vmap(plan)(col_blocks)
    incoming = lax.all_to_all(requests, "grp", split_axis=1, concat_axis=1, tiled=True)

    def answer(source, asked):
        picked = jnp.take(source, jnp.maximum(asked, 0), axis=1)
        return jnp.where((asked >= 0)[None, :, :, None], picked, 0.0)

    replies = jax.vmap(answer)(blocks_own, incoming)
    returned = lax.all_to_all(replies, "grp", split_axis=2, concat_axis=2, tiled=True)
    flat_back = returned.reshape(window_run, fields, groups * slot_count, TILE)
    col_data = jax.vmap(take_blocks)(flat_back, positions)
    same_all = (row_blocks == col_blocks).astype(jnp.float32)
    window = first_window + jnp.arange(window_run, dtype=jnp.int32)
    below = jnp.maximum(window - 1, 0)
    above = jnp.minimum(window + 1, windows - 1)
    lambda_sets = jnp.stack([lambdas[below], lambdas[window], lambdas[above]], axis=1)
    partial_sums = lax.map(
        lambda pack: evaluate(pack[0], pack[1], pack[2], pack[3]),
        (row_data, col_data, same_all, lambda_sets),
    )
    scale_count = listed * groups * TILE * TILE
    lower_win = jnp.where(jnp.remainder(window - parity[0], 2) == 0, window, window - 1)
    upper_win = lower_win + 1
    has_partner = (lower_win >= 0) & (upper_win < windows)
    lower_safe = jnp.clip(lower_win, 0, windows - 1)
    summed = lax.psum(partial_sums, "grp")
    energy = summed / scale_count
    d_plus = energy[:, 2] - energy[:, 1]
    d_minus = energy[:, 0] - energy[:, 1]
    minus_above = from_behind(d_minus[0:1], "win", -1)
    plus_below = from_behind(d_plus[window_run - 1 : window_run], "win", 1)
    minus_next = jnp.concatenate([d_minus[1:], minus_above])
    plus_prev = jnp.concatenate([plus_below, d_plus[:-1]])
    change = jnp.where(lower_win == window, d_plus + minus_next, plus_prev + d_minus)
    carried = entering(jnp.sum(d_plus)[None], "win", add_terms, jnp.zeros((1,), jnp.float32))
    profile = carried + (jnp.cumsum(d_plus) - d_plus)
    offset_draw = jnp.remainder(thresholds[lower_safe] + parity[0], 1073741824) + 1
    draw_share = offset_draw.astype(jnp.float32) / 1073741824.0
    margins = jnp.where(has_partner, -jnp.log(draw_share) - inverse_temp[0] * change, 0.0)
    return (energy, margins, profile)


def solution(mesh):
    return jax.shard_map(
        per_device,
        mesh=mesh,
        in_specs=(P("win", None, "grp"), P("win", "grp"), P("win", "grp"), P(), P(), P(), P()),
        out_specs=(P("win", None), P("win"), P("win")),
        check_vma=False,
    )
```

profile of v0, /device:TPU:1, one launch (start us, length us, event | category | flops | bytes accessed | tf_op | source)
XLA Modules:
  0.0 197.2 jit_solution(12268638286886576941)
XLA Ops:
  0.6 0.7 subtract_add_fusion
  2.1 0.7 copy.51
  2.8 7.4 %all-to-all-start = ((s32[2,16,5]{2,0,1:T(2,128)}), s32[2,16,5]{2,0,1:T(2,128)S(1)}, u32[]{:S(2)}, u32[]{:S(2)}) async-start(s32[2,16,5]{2,0,1:T(2,128)} %copy.51), calls=%async_computation | async-start | bytes 32768 | tf_op jit(solution)/shard_map/all_to_all | solution.py:103
  10.9 0.7 copy-done.5
  11.7 4.7 %all-to-all-done = s32[2,16,5]{2,0,1:T(2,128)S(1)} async-done(((s32[2,16,5]{2,0,1:T(2,128)}), s32[2,16,5]{2,0,1:T(2,128)S(1)}, u32[]{:S(2)}, u32[]{:S(2)}) %all-to-all-start) | async-done | bytes 672 | tf_op jit(solution)/shard_map/all_to_all | solution.py:103
  16.9 1.5 gather_fusion.5
  18.9 1.2 copy.58
  20.1 3.6 %all-to-all-start.1 = ((f32[2,6,16,5,128]{4,0,3,1,2:T(2,128)}), f32[2,6,16,5,128]{4,0,3,1,2:T(2,128)S(1)}, u32[]{:S(2)}, u32[]{:S(2)}) async-start(f32[2,6,16,5,128]{4,0,3,1,2:T(2,128)} %copy.58), calls=%async_computation.1 | async-start | bytes 983040 | tf_op jit(solution)/shard_map/all_to_all | solution.py:110
  23.8 1.0 gather_fusion.4
  29.0 0.7 copy-done.4
  29.7 4.7 %all-to-all-done.1 = f32[2,6,16,5,128]{4,0,3,1,2:T(2,128)S(1)} async-done(((f32[2,6,16,5,128]{4,0,3,1,2:T(2,128)}), f32[2,6,16,5,128]{4,0,3,1,2:T(2,128)S(1)}, u32[]{:S(2)}, u32[]{:S(2)}) %all-to-all-start.1) | async-done | bytes 491552 | tf_op jit(solution)/shard_map/all_to_all | solution.py:110
  34.7 1.0 gather_fusion.6
  36.0 102.3 %while.37 = (s32[]{:T(128)}, f32[2,3]{1,0:T(2,128)S(1)}, f32[2,6,64,128]{3,2,0,1:T(8,128)S(1)}, f32[2,6,64,128]{3,2,0,1:T(8,128)S(1)}, f32[2,64]{1,0:T(2,128)S(1...) while((s32[]{:T(128)}, f32[2,3]{1,0:T(2,128)S(1)}, ...), condition=%wide.region_9.10_spmd, body=%wide.region_3.0_spmd.sunk | while | flops 16812060 | bytes 1377978 | solution.py:118
  36.0 0.7 fusion.47
  38.7 48.4 %while.39 = (s32[]{:T(128)}, f32[3]{0:T(128)S(1)}, f32[3]{0:T(128)S(1)}, f32[64]{0:T(128)S(1)}, f32[6,64,128]{2,1,0:T(8,128)S(1)}, /*index=5*/f32[6,64,128]{2,1,...) while((s32[]{:T(128)}, f32[3]{0:T(128)S(1)}, ...), condition=%wide.region_8.8_spmd.clone, body=%wide.region_4.7_spmd.clone.sunk | while | flops 16812052 | bytes 590521 | solution.py:64
  38.8 0.7 fusion.48
  39.5 4.1 %fusion.50 = (f32[]{:T(128)}, f32[]{:T(128)}) fusion(f32[]{:T(128)} %bitcast.119, f32[16,128]{1,0:T(8,128)S(1)} %get-tuple-element.546, f32[16,128]{1,0:T(8,128)S(1)} %get-tuple-element.547, f32[16,128]{1,0:T(8,128)S(1)} %get-tuple-element.548, f32[16,128]{1,0:T(8,128)S(1)} %get-tuple-element.549, f32[16,128]{1,0:T(8,128)S(1)} %get-tuple-element.550, ...), kind=kLoop, calls=%fused_computation.20.clone.1 | loop fusion | flops 9699326 | bytes 163928 | tf_op jit(solution)/shard_map/while/body/eval_jaxpr/while/body/eval_jaxpr/reduce_sum | solution.py:50
  44.8 3.4 %fusion.51 = f32[]{:T(128)} fusion(f32[]{:T(128)} %bitcast.121, f32[]{:T(128)} %get-tuple-element.604, f32[16,128]{1,0:T(8,128)S(1)} %get-tuple-element.546, f32[16,128]{1,0:T(8,128)S(1)} %get-tuple-element.547, f32[16,128]{1,0:T(8,128)S(1)} %get-tuple-element.548, f32[16,128]{1,0:T(8,128)S(1)} %get-tuple-element.549, ...), kind=kLoop, calls=%fused_computation.23.clone.1 | loop fusion | flops 7077887 | bytes 163916 | tf_op jit(solution)/shard_map/while/body/eval_jaxpr/while/body/eval_jaxpr/reduce_sum | solution.py:50
  50.9 0.7 fusion.48
  51.6 4.1 %fusion.50 = (f32[]{:T(128)}, f32[]{:T(128)}) fusion(f32[]{:T(128)} %bitcast.119, f32[16,128]{1,0:T(8,128)S(1)} %get-tuple-element.546, f32[16,128]{1,0:T(8,128)S(1)} %get-tuple-element.547, f32[16,128]{1,0:T(8,128)S(1)} %get-tuple-element.548, f32[16,128]{1,0:T(8,128)S(1)} %get-tuple-element.549, f32[16,128]{1,0:T(8,128)S(1)} %get-tuple-element.550, ...), kind=kLoop, calls=%fused_computation.20.clone.1 | loop fusion | flops 9699326 | bytes 163928 | tf_op jit(solution)/shard_map/while/body/eval_jaxpr/while/body/eval_jaxpr/reduce_sum | solution.py:50
  56.9 3.4 %fusion.51 = f32[]{:T(128)} fusion(f32[]{:T(128)} %bitcast.121, f32[]{:T(128)} %get-tuple-element.604, f32[16,128]{1,0:T(8,128)S(1)} %get-tuple-element.546, f32[16,128]{1,0:T(8,128)S(1)} %get-tuple-element.547, f32[16,128]{1,0:T(8,128)S(1)} %get-tuple-element.548, f32[16,128]{1,0:T(8,128)S(1)} %get-tuple-element.549, ...), kind=kLoop, calls=%fused_computation.23.clone.1 | loop fusion | flops 7077887 | bytes 163916 | tf_op jit(solution)/shard_map/while/body/eval_jaxpr/while/body/eval_jaxpr/reduce_sum | solution.py:50
  63.0 0.7 fusion.48
  63.7 4.1 %fusion.50 = (f32[]{:T(128)}, f32[]{:T(128)}) fusion(f32[]{:T(128)} %bitcast.119, f32[16,128]{1,0:T(8,128)S(1)} %get-tuple-element.546, f32[16,128]{1,0:T(8,128)S(1)} %get-tuple-element.547, f32[16,128]{1,0:T(8,128)S(1)} %get-tuple-element.548, f32[16,128]{1,0:T(8,128)S(1)} %get-tuple-element.549, f32[16,128]{1,0:T(8,128)S(1)} %get-tuple-element.550, ...), kind=kLoop, calls=%fused_computation.20.clone.1 | loop fusion | flops 9699326 | bytes 163928 | tf_op jit(solution)/shard_map/while/body/eval_jaxpr/while/body/eval_jaxpr/reduce_sum | solution.py:50
  69.0 3.4 %fusion.51 = f32[]{:T(128)} fusion(f32[]{:T(128)} %bitcast.121, f32[]{:T(128)} %get-tuple-element.604, f32[16,128]{1,0:T(8,128)S(1)} %get-tuple-element.546, f32[16,128]{1,0:T(8,128)S(1)} %get-tuple-element.547, f32[16,128]{1,0:T(8,128)S(1)} %get-tuple-element.548, f32[16,128]{1,0:T(8,128)S(1)} %get-tuple-element.549, ...), kind=kLoop, calls=%fused_computation.23.clone.1 | loop fusion | flops 7077887 | bytes 163916 | tf_op jit(solution)/shard_map/while/body/eval_jaxpr/while/body/eval_jaxpr/reduce_sum | solution.py:50
  75.1 0.7 fusion.48
  75.8 4.1 %fusion.50 = (f32[]{:T(128)}, f32[]{:T(128)}) fusion(f32[]{:T(128)} %bitcast.119, f32[16,128]{1,0:T(8,128)S(1)} %get-tuple-element.546, f32[16,128]{1,0:T(8,128)S(1)} %get-tuple-element.547, f32[16,128]{1,0:T(8,128)S(1)} %get-tuple-element.548, f32[16,128]{1,0:T(8,128)S(1)} %get-tuple-element.549, f32[16,128]{1,0:T(8,128)S(1)} %get-tuple-element.550, ...), kind=kLoop, calls=%fused_computation.20.clone.1 | loop fusion | flops 9699326 | bytes 163928 | tf_op jit(solution)/shard_map/while/body/eval_jaxpr/while/body/eval_jaxpr/reduce_sum | solution.py:50
  81.1 3.4 %fusion.51 = f32[]{:T(128)} fusion(f32[]{:T(128)} %bitcast.121, f32[]{:T(128)} %get-tuple-element.604, f32[16,128]{1,0:T(8,128)S(1)} %get-tuple-element.546, f32[16,128]{1,0:T(8,128)S(1)} %get-tuple-element.547, f32[16,128]{1,0:T(8,128)S(1)} %get-tuple-element.548, f32[16,128]{1,0:T(8,128)S(1)} %get-tuple-element.549, ...), kind=kLoop, calls=%fused_computation.23.clone.1 | loop fusion | flops 7077887 | bytes 163916 | tf_op jit(solution)/shard_map/while/body/eval_jaxpr/while/body/eval_jaxpr/reduce_sum | solution.py:50
  87.2 0.7 fusion.47
  89.8 48.4 %while.39 = (s32[]{:T(128)}, f32[3]{0:T(128)S(1)}, f32[3]{0:T(128)S(1)}, f32[64]{0:T(128)S(1)}, f32[6,64,128]{2,1,0:T(8,128)S(1)}, /*index=5*/f32[6,64,128]{2,1,...) while((s32[]{:T(128)}, f32[3]{0:T(128)S(1)}, ...), condition=%wide.region_8.8_spmd.clone, body=%wide.region_4.7_spmd.clone.sunk | while | flops 16812052 | bytes 590521 | solution.py:64
  90.0 0.7 fusion.48
  90.6 4.1 %fusion.50 = (f32[]{:T(128)}, f32[]{:T(128)}) fusion(f32[]{:T(128)} %bitcast.119, f32[16,128]{1,0:T(8,128)S(1)} %get-tuple-element.546, f32[16,128]{1,0:T(8,128)S(1)} %get-tuple-element.547, f32[16,128]{1,0:T(8,128)S(1)} %get-tuple-element.548, f32[16,128]{1,0:T(8,128)S(1)} %get-tuple-element.549, f32[16,128]{1,0:T(8,128)S(1)} %get-tuple-element.550, ...), kind=kLoop, calls=%fused_computation.20.clone.1 | loop fusion | flops 9699326 | bytes 163928 | tf_op jit(solution)/shard_map/while/body/eval_jaxpr/while/body/eval_jaxpr/reduce_sum | solution.py:50
  96.0 3.4 %fusion.51 = f32[]{:T(128)} fusion(f32[]{:T(128)} %bitcast.121, f32[]{:T(128)} %get-tuple-element.604, f32[16,128]{1,0:T(8,128)S(1)} %get-tuple-element.546, f32[16,128]{1,0:T(8,128)S(1)} %get-tuple-element.547, f32[16,128]{1,0:T(8,128)S(1)} %get-tuple-element.548, f32[16,128]{1,0:T(8,128)S(1)} %get-tuple-element.549, ...), kind=kLoop, calls=%fused_computation.23.clone.1 | loop fusion | flops 7077887 | bytes 163916 | tf_op jit(solution)/shard_map/while/body/eval_jaxpr/while/body/eval_jaxpr/reduce_sum | solution.py:50
  102.1 0.7 fusion.48
  102.7 4.1 %fusion.50 = (f32[]{:T(128)}, f32[]{:T(128)}) fusion(f32[]{:T(128)} %bitcast.119, f32[16,128]{1,0:T(8,128)S(1)} %get-tuple-element.546, f32[16,128]{1,0:T(8,128)S(1)} %get-tuple-element.547, f32[16,128]{1,0:T(8,128)S(1)} %get-tuple-element.548, f32[16,128]{1,0:T(8,128)S(1)} %get-tuple-element.549, f32[16,128]{1,0:T(8,128)S(1)} %get-tuple-element.550, ...), kind=kLoop, calls=%fused_computation.20.clone.1 | loop fusion | flops 9699326 | bytes 163928 | tf_op jit(solution)/shard_map/while/body/eval_jaxpr/while/body/eval_jaxpr/reduce_sum | solution.py:50
  108.1 3.4 %fusion.51 = f32[]{:T(128)} fusion(f32[]{:T(128)} %bitcast.121, f32[]{:T(128)} %get-tuple-element.604, f32[16,128]{1,0:T(8,128)S(1)} %get-tuple-element.546, f32[16,128]{1,0:T(8,128)S(1)} %get-tuple-element.547, f32[16,128]{1,0:T(8,128)S(1)} %get-tuple-element.548, f32[16,128]{1,0:T(8,128)S(1)} %get-tuple-element.549, ...), kind=kLoop, calls=%fused_computation.23.clone.1 | loop fusion | flops 7077887 | bytes 163916 | tf_op jit(solution)/shard_map/while/body/eval_jaxpr/while/body/eval_jaxpr/reduce_sum | solution.py:50
  114.2 0.7 fusion.48
  114.8 4.1 %fusion.50 = (f32[]{:T(128)}, f32[]{:T(128)}) fusion(f32[]{:T(128)} %bitcast.119, f32[16,128]{1,0:T(8,128)S(1)} %get-tuple-element.546, f32[16,128]{1,0:T(8,128)S(1)} %get-tuple-element.547, f32[16,128]{1,0:T(8,128)S(1)} %get-tuple-element.548, f32[16,128]{1,0:T(8,128)S(1)} %get-tuple-element.549, f32[16,128]{1,0:T(8,128)S(1)} %get-tuple-element.550, ...), kind=kLoop, calls=%fused_computation.20.clone.1 | loop fusion | flops 9699326 | bytes 163928 | tf_op jit(solution)/shard_map/while/body/eval_jaxpr/while/body/eval_jaxpr/reduce_sum | solution.py:50
  120.1 3.4 %fusion.51 = f32[]{:T(128)} fusion(f32[]{:T(128)} %bitcast.121, f32[]{:T(128)} %get-tuple-element.604, f32[16,128]{1,0:T(8,128)S(1)} %get-tuple-element.546, f32[16,128]{1,0:T(8,128)S(1)} %get-tuple-element.547, f32[16,128]{1,0:T(8,128)S(1)} %get-tuple-element.548, f32[16,128]{1,0:T(8,128)S(1)} %get-tuple-element.549, ...), kind=kLoop, calls=%fused_computation.23.clone.1 | loop fusion | flops 7077887 | bytes 163916 | tf_op jit(solution)/shard_map/while/body/eval_jaxpr/while/body/eval_jaxpr/reduce_sum | solution.py:50
  126.9 4.1 %fusion.50 = (f32[]{:T(128)}, f32[]{:T(128)}) fusion(f32[]{:T(128)} %bitcast.119, f32[16,128]{1,0:T(8,128)S(1)} %get-tuple-element.546, f32[16,128]{1,0:T(8,128)S(1)} %get-tuple-element.547, f32[16,128]{1,0:T(8,128)S(1)} %get-tuple-element.548, f32[16,128]{1,0:T(8,128)S(1)} %get-tuple-element.549, f32[16,128]{1,0:T(8,128)S(1)} %get-tuple-element.550, ...), kind=kLoop, calls=%fused_computation.20.clone.1 | loop fusion | flops 9699326 | bytes 163928 | tf_op jit(solution)/shard_map/while/body/eval_jaxpr/while/body/eval_jaxpr/reduce_sum | solution.py:50
  132.2 3.4 %fusion.51 = f32[]{:T(128)} fusion(f32[]{:T(128)} %bitcast.121, f32[]{:T(128)} %get-tuple-element.604, f32[16,128]{1,0:T(8,128)S(1)} %get-tuple-element.546, f32[16,128]{1,0:T(8,128)S(1)} %get-tuple-element.547, f32[16,128]{1,0:T(8,128)S(1)} %get-tuple-element.548, f32[16,128]{1,0:T(8,128)S(1)} %get-tuple-element.549, ...), kind=kLoop, calls=%fused_computation.23.clone.1 | loop fusion | flops 7077887 | bytes 163916 | tf_op jit(solution)/shard_map/while/body/eval_jaxpr/while/body/eval_jaxpr/reduce_sum | solution.py:50
  138.3 34.5 %psum.7 = f32[2,3]{1,0:T(2,128)S(1)} all-reduce(f32[2,3]{1,0:T(2,128)S(1)} %get-tuple-element.224), channel_id=1, replica_groups=mesh['win'=2,'grp'=16] {'grp'}, use_global_device_ids=true, to_apply=%region_10.11 | all-reduce | flops 6 | bytes 48 | tf_op jit(solution)/shard_map/psum | solution.py:127
  172.8 0.7 fusion.31
  174.1 11.6 %collective-permute-start = (f32[1]{0:T(128)}, f32[1]{0:T(128)}, u32[]{:S(2)}, u32[]{:S(2)}) collective-permute-start(f32[1]{0:T(128)} %bitcast.29), channel_id=1, source_target_pairs={{16,0},{17,1},{18,2},{19,3},{20,4},{21,5},{22,6},{23,7},{24,8},{25... | collective-permute-start | bytes 20 | tf_op jit(solution)/shard_map/ppermute | solution.py:13
  186.2 1.4 dynamic-update-slice
  187.6 1.3 collective-permute-start.1
  188.9 3.8 %all-reduce = f32[2]{0:T(128)S(1)} all-reduce(f32[2]{0:T(128)S(1)} %dynamic-update-slice), channel_id=1, replica_groups=mesh['win'=2,'grp'=16] {'win'}, use_global_device_ids=true, to_apply=%add | all-reduce | flops 2 | bytes 16
  192.7 1.2 while.38
  194.1 3.1 %subtract_add_fusion.1 = (f32[2]{0:T(128)}, f32[2]{0:T(128)}) fusion(f32[2]{0:T(128)S(1)} %reduce.3, f32[2]{0:T(128)S(1)} %get-tuple-element.365, f32[]{:T(128)} %bitcast.35, f32[2]{0:T(128)S(1)} %get-tuple-element.328, f32[1]{0:T(128)} %bitcast.31, f32[1]{0:T(128)} %collective-permute-done.1, f32[1]{0:T(128)} %collective-permute-done, f32[1]{0:T(128)} %bitcast.28, ...), kind=kLoop, calls=%fused_computation.115 | loop fusion | flops 94 | bytes 80 | tf_op jit(solution)/shard_map/add | solution.py:137
  (108 shorter events, 10.4 us)
Async XLA Ops:
  0.6 24.3 %copy-start = (f32[4]{0:T(128)S(1)}, f32[4]{0:T(128)}, u32[]{:S(2)}) copy-start(f32[4]{0:T(128)} %param.16) | copy-start | bytes 52
  1.8 9.8 %copy-start.2 = (f32[2,6,1536]{2,0,1:T(2,128)S(1)}, f32[2,6,1536]{2,0,1:T(2,128)}, u32[]{:S(2)}) copy-start(f32[2,6,1536]{2,0,1:T(2,128)} %param.13) | copy-start | bytes 221188
  2.8 13.6 %all-to-all-start = ((s32[2,16,5]{2,0,1:T(2,128)}), s32[2,16,5]{2,0,1:T(2,128)S(1)}, u32[]{:S(2)}, u32[]{:S(2)}) async-start(s32[2,16,5]{2,0,1:T(2,128)} %copy.51), calls=%async_computation | async-start | bytes 32768 | tf_op jit(solution)/shard_map/all_to_all | solution.py:103
  10.8 0.7 copy-start.5
  20.1 14.3 %all-to-all-start.1 = ((f32[2,6,16,5,128]{4,0,3,1,2:T(2,128)}), f32[2,6,16,5,128]{4,0,3,1,2:T(2,128)S(1)}, u32[]{:S(2)}, u32[]{:S(2)}) async-start(f32[2,6,16,5,128]{4,0,3,1,2:T(2,128)} %copy.58), calls=%async_computation.1 | async-start | bytes 983040 | tf_op jit(solution)/shard_map/all_to_all | solution.py:110
  26.2 2.1 %copy-start.1 = (s32[4]{0:T(128)S(1)}, s32[4]{0:T(128)}, u32[]{:S(2)}) copy-start(s32[4]{0:T(128)} %param.19) | copy-start | bytes 52
  27.0 0.7 copy-start.6
  29.0 0.7 copy-start.4
  172.8 0.7 copy-start.3
  174.1 20.0 %collective-permute-start = (f32[1]{0:T(128)}, f32[1]{0:T(128)}, u32[]{:S(2)}, u32[]{:S(2)}) collective-permute-start(f32[1]{0:T(128)} %bitcast.29), channel_id=1, source_target_pairs={{16,0},{17,1},{18,2},{19,3},{20,4},{21,5},{22,6},{23,7},{24,8},{25... | collective-permute-start | bytes 20 | tf_op jit(solution)/shard_map/ppermute | solution.py:13
  187.6 6.5 %collective-permute-start.1 = (f32[1]{0:T(128)}, f32[1]{0:T(128)}, u32[]{:S(2)}, u32[]{:S(2)}) collective-permute-start(f32[1]{0:T(128)} %bitcast.30), channel_id=1, source_target_pairs={{0,16},{1,17},{2,18},{3,19},{4,20},{5,21},{6,22},{7,23},{8,24},{9,... | collective-permute-start | bytes 20 | tf_op jit(solution)/shard_map/ppermute | solution.py:13
where the time goes:
time: 198 us; the launch traced here: 197 us
  other arithmetic  66.4 us (34%)
  blocking collectives  38.3 us (19%)
  loops' own time  35.2 us (18%)
  starting transfers between devices  23.8 us (12%)
  local copies, waits for them, and re-layouts  22 us (11%)
  waiting for transfers between devices  9.33 us (5%)
  between operations  2.23 us (1%)
    reduce_sum x16, other arithmetic, pair_energy(): totals.append(lam_now * jnp.sum(keep_mask * (dispersion + coulomb)))  59.4 us
    psum x1, blocking collectives, per_device(): summed = lax.psum(partial_sums, 'grp')  34.5 us
    another operation x2, loops' own time, evaluate(): return lax.fori_loop(0, count, advance, jnp.zeros((3,), jnp.float32))  30.6 us
    ppermute x2, starting transfers between devices, from_behind(): return lax.ppermute(shard, axis, pairs)  12.9 us
    all_to_all x1, starting transfers between devices, per_device(): lax.all_to_all(requests, 'grp', split_axis=1, concat_axis=1, tiled=True)  7.4 us
    slice x10, local copies, waits for them, and re-layouts, pair_energy(): lam_now = lambda_set[number]  6.66 us
    all_to_all x1, waiting for transfers between devices, per_device(): lax.all_to_all(replies, 'grp', split_axis=2, concat_axis=2, tiled=True)  4.67 us
    all_to_all x1, waiting for transfers between devices, per_device(): lax.all_to_all(requests, 'grp', split_axis=1, concat_axis=1, tiled=True)  4.66 us
  transfers between devices with their start and end apart: 4, of which 2 were waited for; matrix products, arithmetic and copies ran while one was open for 4% of the time, Pallas kernels for 0%

commit v1 on v0

--- a/solution.py
+++ b/solution.py
@@ -5,6 +5,37 @@
 
 TILE = 128
 tiles_per_step = 16
+
+
+def state_halves(local_block, array_axis, w_in):
+    mat_out = local_block.shape
+    out_arr = local_block.reshape(
+        *mat_out[:array_axis], w_in, mat_out[array_axis] // w_in, *mat_out[array_axis + 1 :]
+    )
+    vec_out = jnp.moveaxis(out_arr, array_axis, 0)
+    return vec_out
+
+
+def play_the_rates(base_x, at_axis):
+    local_now = list(base_x.shape[1:])
+    local_now[at_axis] *= base_x.shape[0]
+    found_now = jnp.moveaxis(base_x, 0, at_axis).reshape(local_now)
+    return found_now
+
+
+def process_strips_all(local, a_name, array_here, u):
+    all_values = jax.lax.axis_size(a_name)
+    y2, moved = (all_values, jax.lax.axis_index(a_name))
+    arr_now = state_halves(local, array_here, y2)
+    rack = [arr_now[moved]]
+    q = 1
+    while q < y2:
+        right_arr = arr_now[moved ^ q]
+        rack.append(jax.lax.ppermute(right_arr, a_name, [(num, num ^ q) for num in range(y2)]))
+        q += 1
+    arr_now = jnp.stack(rack)[moved ^ jnp.arange(y2)]
+    outcome_arr = play_the_rates(arr_now, u)
+    return outcome_arr
 
 
 def from_behind(shard, axis, by):
@@ -100,7 +131,7 @@
         return (owner_ids * slot_count + order_rank, requests)
 
     positions, requests = jax.vmap(plan)(col_blocks)
-    incoming = lax.all_to_all(requests, "grp", split_axis=1, concat_axis=1, tiled=True)
+    incoming = process_strips_all(requests, "grp", 1, 1)
 
     def answer(source, asked):
         picked = jnp.take(source, jnp.maximum(asked, 0), axis=1)

time: 198 us -> 218 us (1.10)
  starting transfers between devices: 23.8 us -> 45.3 us
  blocking collectives: 38.3 us -> 35.6 us
    ppermute x0 -> x15, starting transfers between devices: none -> 23.9 us  [process_strips_all(): jax.lax.ppermute(right_arr, a_name, [(num, num ^ q) for num in range(y2)])]
    all_to_all x1 -> x0, starting transfers between devices: 7.4 us -> none  [per_device(): lax.all_to_all(requests, 'grp', split_axis=1, concat_axis=1, tiled=True)]
    ppermute x0 -> x15, waiting for transfers between devices: none -> 5.48 us  [process_strips_all(): jax.lax.ppermute(right_arr, a_name, [(num, num ^ q) for num in range(y2)])]
    ppermute x2, starting transfers between devices: 12.9 us -> 17.8 us  [from_behind(): return lax.ppermute(shard, axis, pairs)]
    all_to_all x1 -> x0, waiting for transfers between devices: 4.66 us -> none  [per_device(): lax.all_to_all(requests, 'grp', split_axis=1, concat_axis=1, tiled=True)]
    psum x1, blocking collectives: 34.5 us -> 31.8 us  [per_device(): summed = lax.psum(partial_sums, 'grp')]
  transfers between devices with their start and end apart: 4 -> 18, of which waited for: 2 -> 3; matrix products, arithmetic and copies ran while one was open for 4% -> 4% of each run, Pallas kernels for 0% -> 0%
where the time goes in v1:
time: 218 us; the launch traced here: 217 us
  other arithmetic  67.3 us (31%)
  starting transfers between devices  45.3 us (21%)
  blocking collectives  35.6 us (16%)
  loops' own time  35.1 us (16%)
  local copies, waits for them, and re-layouts  21.9 us (10%)
  waiting for transfers between devices  9.44 us (4%)
  between operations  2.66 us (1%)
    reduce_sum x16, other arithmetic, pair_energy(): totals.append(lam_now * jnp.sum(keep_mask * (dispersion + coulomb)))  59.4 us
    psum x1, blocking collectives, per_device(): summed = lax.psum(partial_sums, 'grp')  31.8 us
    another operation x2, loops' own time, evaluate(): return lax.fori_loop(0, count, advance, jnp.zeros((3,), jnp.float32))  30.6 us
    ppermute x15, starting transfers between devices, process_strips_all(): jax.lax.ppermute(right_arr, a_name, [(num, num ^ q) for num in range(y2)])  23.9 us
    ppermute x2, starting transfers between devices, from_behind(): return lax.ppermute(shard, axis, pairs)  17.8 us
    slice x10, local copies, waits for them, and re-layouts, pair_energy(): lam_now = lambda_set[number]  6.66 us
    ppermute x15, waiting for transfers between devices, process_strips_all(): jax.lax.ppermute(right_arr, a_name, [(num, num ^ q) for num in range(y2)])  5.48 us
  transfers between devices with their start and end apart: 18, of which 3 were waited for; matrix products, arithmetic and copies ran while one was open for 4% of the time, Pallas kernels for 0%

profile of v1, /device:TPU:1, one launch (start us, length us, event | category | flops | bytes accessed | tf_op | source)
XLA Modules:
  0.0 217.3 jit_solution(13309397440371328471)
XLA Ops:
  0.7 0.7 copy-done.4
  2.5 2.1 collective-permute-start
  4.5 1.2 collective-permute-start.1
  5.8 1.5 collective-permute-start.3
  7.3 1.1 collective-permute-start.4
  9.9 2.3 %collective-permute-start.5 = (s32[2,1,5]{1,2,0:T(8,128)S(1)}, s32[2,1,5]{1,2,0:T(8,128)S(1)}, u32[]{:S(2)}, u32[]{:S(2)}) collective-permute-start(s32[2,1,5]{1,2,0:T(8,128)S(1)} %get-tuple-element.376), channel_id=1, source_target_pairs={{0,6},{1,7},{2,4},{3,5},{4,2},{5,3},{6,0},{7,1},{8,14},{9,15},{10,... | collective-permute-start | bytes 128 | tf_op jit(solution)/shard_map/ppermute | solution.py:34
  12.6 2.4 %collective-permute-start.7 = (s32[2,1,5]{1,2,0:T(8,128)S(1)}, s32[2,1,5]{1,2,0:T(8,128)S(1)}, u32[]{:S(2)}, u32[]{:S(2)}) collective-permute-start(s32[2,1,5]{1,2,0:T(8,128)S(1)} %get-tuple-element.374), channel_id=1, source_target_pairs={{0,8},{1,9},{2,10},{3,11},{4,12},{5,13},{6,14},{7,15},{8,0},{9,1},... | collective-permute-start | bytes 128 | tf_op jit(solution)/shard_map/ppermute | solution.py:34
  15.2 1.0 collective-permute-start.8
  16.3 3.3 %collective-permute-start.9 = (s32[2,1,5]{1,2,0:T(8,128)S(1)}, s32[2,1,5]{1,2,0:T(8,128)S(1)}, u32[]{:S(2)}, u32[]{:S(2)}) collective-permute-start(s32[2,1,5]{1,2,0:T(8,128)S(1)} %get-tuple-element.372), channel_id=1, source_target_pairs={{0,10},{1,11},{2,8},{3,9},{4,14},{5,15},{6,12},{7,13},{8,2},{9,3},... | collective-permute-start | bytes 128 | tf_op jit(solution)/shard_map/ppermute | solution.py:34
  20.0 3.3 %collective-permute-start.11 = (s32[2,1,5]{1,2,0:T(8,128)S(1)}, s32[2,1,5]{1,2,0:T(8,128)S(1)}, u32[]{:S(2)}, u32[]{:S(2)}) collective-permute-start(s32[2,1,5]{1,2,0:T(8,128)S(1)} %get-tuple-element.370), channel_id=1, source_target_pairs={{0,12},{1,13},{2,14},{3,15},{4,8},{5,9},{6,10},{7,11},{8,4},{9,5},... | collective-permute-start | bytes 128 | tf_op jit(solution)/shard_map/ppermute | solution.py:34
  23.5 1.0 collective-permute-start.12
  24.6 4.3 %collective-permute-start.13 = (s32[2,1,5]{1,2,0:T(8,128)S(1)}, s32[2,1,5]{1,2,0:T(8,128)S(1)}, u32[]{:S(2)}, u32[]{:S(2)}) collective-permute-start(s32[2,1,5]{1,2,0:T(8,128)S(1)} %get-tuple-element.368), channel_id=1, source_target_pairs={{0,14},{1,15},{2,12},{3,13},{4,10},{5,11},{6,8},{7,9},{8,6},{9,7},... | collective-permute-start | bytes 128 | tf_op jit(solution)/shard_map/ppermute | solution.py:34
  30.1 5.1 %collective-permute-done.14 = s32[2,1,5]{1,2,0:T(8,128)S(1)} collective-permute-done((s32[2,1,5]{1,2,0:T(8,128)S(1)}, s32[2,1,5]{1,2,0:T(8,128)S(1)}, u32[]{:S(2)}, u32[]{:S(2)}) %collective-permute-start.14) | collective-permute-done | bytes 72 | tf_op jit(solution)/shard_map/ppermute | solution.py:34
  36.1 1.5 gather_fusion.6
  38.1 1.2 copy.137
  39.3 3.6 %all-to-all-start = ((f32[2,6,16,5,128]{4,0,3,1,2:T(2,128)}), f32[2,6,16,5,128]{4,0,3,1,2:T(2,128)S(1)}, u32[]{:S(2)}, u32[]{:S(2)}) async-start(f32[2,6,16,5,128]{4,0,3,1,2:T(2,128)} %copy.137), calls=%async_computation | async-start | bytes 983040 | tf_op jit(solution)/shard_map/all_to_all | solution.py:141
  43.0 1.0 gather_fusion.5
  48.2 4.0 %all-to-all-done = f32[2,6,16,5,128]{4,0,3,1,2:T(2,128)S(1)} async-done(((f32[2,6,16,5,128]{4,0,3,1,2:T(2,128)}), f32[2,6,16,5,128]{4,0,3,1,2:T(2,128)S(1)}, u32[]{:S(2)}, u32[]{:S(2)}) %all-to-all-start) | async-done | bytes 491552 | tf_op jit(solution)/shard_map/all_to_all | solution.py:141
  52.5 1.0 gather_fusion.7
  53.8 102.3 %while.37 = (s32[]{:T(128)}, f32[2,3]{1,0:T(2,128)S(1)}, f32[2,6,64,128]{3,2,0,1:T(8,128)S(1)}, f32[2,6,64,128]{3,2,0,1:T(8,128)S(1)}, f32[2,64]{1,0:T(2,128)S(1...) while((s32[]{:T(128)}, f32[2,3]{1,0:T(2,128)S(1)}, ...), condition=%wide.region_9.10_spmd, body=%wide.region_3.0_spmd.sunk | while | flops 16812060 | bytes 1377978 | solution.py:149
  53.9 0.7 fusion.48
  56.5 48.4 %while.39 = (s32[]{:T(128)}, f32[3]{0:T(128)S(1)}, f32[3]{0:T(128)S(1)}, f32[64]{0:T(128)S(1)}, f32[6,64,128]{2,1,0:T(8,128)S(1)}, /*index=5*/f32[6,64,128]{2,1,...) while((s32[]{:T(128)}, f32[3]{0:T(128)S(1)}, ...), condition=%wide.region_8.8_spmd.clone, body=%wide.region_4.7_spmd.clone.sunk | while | flops 16812052 | bytes 590521 | solution.py:95
  57.3 4.1 %fusion.51 = (f32[]{:T(128)}, f32[]{:T(128)}) fusion(f32[]{:T(128)} %bitcast.202, f32[16,128]{1,0:T(8,128)S(1)} %get-tuple-element.568, f32[16,128]{1,0:T(8,128)S(1)} %get-tuple-element.569, f32[16,128]{1,0:T(8,128)S(1)} %get-tuple-element.570, f32[16,128]{1,0:T(8,128)S(1)} %get-tuple-element.571, f32[16,128]{1,0:T(8,128)S(1)} %get-tuple-element.572, ...), kind=kLoop, calls=%fused_computation.21.clone.1 | loop fusion | flops 9699326 | bytes 163928 | tf_op jit(solution)/shard_map/while/body/eval_jaxpr/while/body/eval_jaxpr/reduce_sum | solution.py:81
  62.6 3.4 %fusion.52 = f32[]{:T(128)} fusion(f32[]{:T(128)} %bitcast.204, f32[]{:T(128)} %get-tuple-element.626, f32[16,128]{1,0:T(8,128)S(1)} %get-tuple-element.568, f32[16,128]{1,0:T(8,128)S(1)} %get-tuple-element.569, f32[16,128]{1,0:T(8,128)S(1)} %get-tuple-element.570, f32[16,128]{1,0:T(8,128)S(1)} %get-tuple-element.571, ...), kind=kLoop, calls=%fused_computation.24.clone.1 | loop fusion | flops 7077887 | bytes 163916 | tf_op jit(solution)/shard_map/while/body/eval_jaxpr/while/body/eval_jaxpr/reduce_sum | solution.py:81
  69.4 4.1 %fusion.51 = (f32[]{:T(128)}, f32[]{:T(128)}) fusion(f32[]{:T(128)} %bitcast.202, f32[16,128]{1,0:T(8,128)S(1)} %get-tuple-element.568, f32[16,128]{1,0:T(8,128)S(1)} %get-tuple-element.569, f32[16,128]{1,0:T(8,128)S(1)} %get-tuple-element.570, f32[16,128]{1,0:T(8,128)S(1)} %get-tuple-element.571, f32[16,128]{1,0:T(8,128)S(1)} %get-tuple-element.572, ...), kind=kLoop, calls=%fused_computation.21.clone.1 | loop fusion | flops 9699326 | bytes 163928 | tf_op jit(solution)/shard_map/while/body/eval_jaxpr/while/body/eval_jaxpr/reduce_sum | solution.py:81
  74.7 3.4 %fusion.52 = f32[]{:T(128)} fusion(f32[]{:T(128)} %bitcast.204, f32[]{:T(128)} %get-tuple-element.626, f32[16,128]{1,0:T(8,128)S(1)} %get-tuple-element.568, f32[16,128]{1,0:T(8,128)S(1)} %get-tuple-element.569, f32[16,128]{1,0:T(8,128)S(1)} %get-tuple-element.570, f32[16,128]{1,0:T(8,128)S(1)} %get-tuple-element.571, ...), kind=kLoop, calls=%fused_computation.24.clone.1 | loop fusion | flops 7077887 | bytes 163916 | tf_op jit(solution)/shard_map/while/body/eval_jaxpr/while/body/eval_jaxpr/reduce_sum | solution.py:81
  81.5 4.1 %fusion.51 = (f32[]{:T(128)}, f32[]{:T(128)}) fusion(f32[]{:T(128)} %bitcast.202, f32[16,128]{1,0:T(8,128)S(1)} %get-tuple-element.568, f32[16,128]{1,0:T(8,128)S(1)} %get-tuple-element.569, f32[16,128]{1,0:T(8,128)S(1)} %get-tuple-element.570, f32[16,128]{1,0:T(8,128)S(1)} %get-tuple-element.571, f32[16,128]{1,0:T(8,128)S(1)} %get-tuple-element.572, ...), kind=kLoop, calls=%fused_computation.21.clone.1 | loop fusion | flops 9699326 | bytes 163928 | tf_op jit(solution)/shard_map/while/body/eval_jaxpr/while/body/eval_jaxpr/reduce_sum | solution.py:81
  86.8 3.4 %fusion.52 = f32[]{:T(128)} fusion(f32[]{:T(128)} %bitcast.204, f32[]{:T(128)} %get-tuple-element.626, f32[16,128]{1,0:T(8,128)S(1)} %get-tuple-element.568, f32[16,128]{1,0:T(8,128)S(1)} %get-tuple-element.569, f32[16,128]{1,0:T(8,128)S(1)} %get-tuple-element.570, f32[16,128]{1,0:T(8,128)S(1)} %get-tuple-element.571, ...), kind=kLoop, calls=%fused_computation.24.clone.1 | loop fusion | flops 7077887 | bytes 163916 | tf_op jit(solution)/shard_map/while/body/eval_jaxpr/while/body/eval_jaxpr/reduce_sum | solution.py:81
  93.6 4.1 %fusion.51 = (f32[]{:T(128)}, f32[]{:T(128)}) fusion(f32[]{:T(128)} %bitcast.202, f32[16,128]{1,0:T(8,128)S(1)} %get-tuple-element.568, f32[16,128]{1,0:T(8,128)S(1)} %get-tuple-element.569, f32[16,128]{1,0:T(8,128)S(1)} %get-tuple-element.570, f32[16,128]{1,0:T(8,128)S(1)} %get-tuple-element.571, f32[16,128]{1,0:T(8,128)S(1)} %get-tuple-element.572, ...), kind=kLoop, calls=%fused_computation.21.clone.1 | loop fusion | flops 9699326 | bytes 163928 | tf_op jit(solution)/shard_map/while/body/eval_jaxpr/while/body/eval_jaxpr/reduce_sum | solution.py:81
  98.9 3.4 %fusion.52 = f32[]{:T(128)} fusion(f32[]{:T(128)} %bitcast.204, f32[]{:T(128)} %get-tuple-element.626, f32[16,128]{1,0:T(8,128)S(1)} %get-tuple-element.568, f32[16,128]{1,0:T(8,128)S(1)} %get-tuple-element.569, f32[16,128]{1,0:T(8,128)S(1)} %get-tuple-element.570, f32[16,128]{1,0:T(8,128)S(1)} %get-tuple-element.571, ...), kind=kLoop, calls=%fused_computation.24.clone.1 | loop fusion | flops 7077887 | bytes 163916 | tf_op jit(solution)/shard_map/while/body/eval_jaxpr/while/body/eval_jaxpr/reduce_sum | solution.py:81
  105.0 0.7 fusion.48
  107.7 48.4 %while.39 = (s32[]{:T(128)}, f32[3]{0:T(128)S(1)}, f32[3]{0:T(128)S(1)}, f32[64]{0:T(128)S(1)}, f32[6,64,128]{2,1,0:T(8,128)S(1)}, /*index=5*/f32[6,64,128]{2,1,...) while((s32[]{:T(128)}, f32[3]{0:T(128)S(1)}, ...), condition=%wide.region_8.8_spmd.clone, body=%wide.region_4.7_spmd.clone.sunk | while | flops 16812052 | bytes 590521 | solution.py:95
  108.5 4.1 %fusion.51 = (f32[]{:T(128)}, f32[]{:T(128)}) fusion(f32[]{:T(128)} %bitcast.202, f32[16,128]{1,0:T(8,128)S(1)} %get-tuple-element.568, f32[16,128]{1,0:T(8,128)S(1)} %get-tuple-element.569, f32[16,128]{1,0:T(8,128)S(1)} %get-tuple-element.570, f32[16,128]{1,0:T(8,128)S(1)} %get-tuple-element.571, f32[16,128]{1,0:T(8,128)S(1)} %get-tuple-element.572, ...), kind=kLoop, calls=%fused_computation.21.clone.1 | loop fusion | flops 9699326 | bytes 163928 | tf_op jit(solution)/shard_map/while/body/eval_jaxpr/while/body/eval_jaxpr/reduce_sum | solution.py:81
  113.8 3.4 %fusion.52 = f32[]{:T(128)} fusion(f32[]{:T(128)} %bitcast.204, f32[]{:T(128)} %get-tuple-element.626, f32[16,128]{1,0:T(8,128)S(1)} %get-tuple-element.568, f32[16,128]{1,0:T(8,128)S(1)} %get-tuple-element.569, f32[16,128]{1,0:T(8,128)S(1)} %get-tuple-element.570, f32[16,128]{1,0:T(8,128)S(1)} %get-tuple-element.571, ...), kind=kLoop, calls=%fused_computation.24.clone.1 | loop fusion | flops 7077887 | bytes 163916 | tf_op jit(solution)/shard_map/while/body/eval_jaxpr/while/body/eval_jaxpr/reduce_sum | solution.py:81
  120.6 4.1 %fusion.51 = (f32[]{:T(128)}, f32[]{:T(128)}) fusion(f32[]{:T(128)} %bitcast.202, f32[16,128]{1,0:T(8,128)S(1)} %get-tuple-element.568, f32[16,128]{1,0:T(8,128)S(1)} %get-tuple-element.569, f32[16,128]{1,0:T(8,128)S(1)} %get-tuple-element.570, f32[16,128]{1,0:T(8,128)S(1)} %get-tuple-element.571, f32[16,128]{1,0:T(8,128)S(1)} %get-tuple-element.572, ...), kind=kLoop, calls=%fused_computation.21.clone.1 | loop fusion | flops 9699326 | bytes 163928 | tf_op jit(solution)/shard_map/while/body/eval_jaxpr/while/body/eval_jaxpr/reduce_sum | solution.py:81
  125.9 3.4 %fusion.52 = f32[]{:T(128)} fusion(f32[]{:T(128)} %bitcast.204, f32[]{:T(128)} %get-tuple-element.626, f32[16,128]{1,0:T(8,128)S(1)} %get-tuple-element.568, f32[16,128]{1,0:T(8,128)S(1)} %get-tuple-element.569, f32[16,128]{1,0:T(8,128)S(1)} %get-tuple-element.570, f32[16,128]{1,0:T(8,128)S(1)} %get-tuple-element.571, ...), kind=kLoop, calls=%fused_computation.24.clone.1 | loop fusion | flops 7077887 | bytes 163916 | tf_op jit(solution)/shard_map/while/body/eval_jaxpr/while/body/eval_jaxpr/reduce_sum | solution.py:81
  132.7 4.1 %fusion.51 = (f32[]{:T(128)}, f32[]{:T(128)}) fusion(f32[]{:T(128)} %bitcast.202, f32[16,128]{1,0:T(8,128)S(1)} %get-tuple-element.568, f32[16,128]{1,0:T(8,128)S(1)} %get-tuple-element.569, f32[16,128]{1,0:T(8,128)S(1)} %get-tuple-element.570, f32[16,128]{1,0:T(8,128)S(1)} %get-tuple-element.571, f32[16,128]{1,0:T(8,128)S(1)} %get-tuple-element.572, ...), kind=kLoop, calls=%fused_computation.21.clone.1 | loop fusion | flops 9699326 | bytes 163928 | tf_op jit(solution)/shard_map/while/body/eval_jaxpr/while/body/eval_jaxpr/reduce_sum | solution.py:81
  138.0 3.4 %fusion.52 = f32[]{:T(128)} fusion(f32[]{:T(128)} %bitcast.204, f32[]{:T(128)} %get-tuple-element.626, f32[16,128]{1,0:T(8,128)S(1)} %get-tuple-element.568, f32[16,128]{1,0:T(8,128)S(1)} %get-tuple-element.569, f32[16,128]{1,0:T(8,128)S(1)} %get-tuple-element.570, f32[16,128]{1,0:T(8,128)S(1)} %get-tuple-element.571, ...), kind=kLoop, calls=%fused_computation.24.clone.1 | loop fusion | flops 7077887 | bytes 163916 | tf_op jit(solution)/shard_map/while/body/eval_jaxpr/while/body/eval_jaxpr/reduce_sum | solution.py:81
  144.8 4.1 %fusion.51 = (f32[]{:T(128)}, f32[]{:T(128)}) fusion(f32[]{:T(128)} %bitcast.202, f32[16,128]{1,0:T(8,128)S(1)} %get-tuple-element.568, f32[16,128]{1,0:T(8,128)S(1)} %get-tuple-element.569, f32[16,128]{1,0:T(8,128)S(1)} %get-tuple-element.570, f32[16,128]{1,0:T(8,128)S(1)} %get-tuple-element.571, f32[16,128]{1,0:T(8,128)S(1)} %get-tuple-element.572, ...), kind=kLoop, calls=%fused_computation.21.clone.1 | loop fusion | flops 9699326 | bytes 163928 | tf_op jit(solution)/shard_map/while/body/eval_jaxpr/while/body/eval_jaxpr/reduce_sum | solution.py:81
  150.1 3.4 %fusion.52 = f32[]{:T(128)} fusion(f32[]{:T(128)} %bitcast.204, f32[]{:T(128)} %get-tuple-element.626, f32[16,128]{1,0:T(8,128)S(1)} %get-tuple-element.568, f32[16,128]{1,0:T(8,128)S(1)} %get-tuple-element.569, f32[16,128]{1,0:T(8,128)S(1)} %get-tuple-element.570, f32[16,128]{1,0:T(8,128)S(1)} %get-tuple-element.571, ...), kind=kLoop, calls=%fused_computation.24.clone.1 | loop fusion | flops 7077887 | bytes 163916 | tf_op jit(solution)/shard_map/while/body/eval_jaxpr/while/body/eval_jaxpr/reduce_sum | solution.py:81
  156.1 31.8 %psum.7 = f32[2,3]{1,0:T(2,128)S(1)} all-reduce(f32[2,3]{1,0:T(2,128)S(1)} %get-tuple-element.224), channel_id=1, replica_groups=mesh['win'=2,'grp'=16] {'grp'}, use_global_device_ids=true, to_apply=%region_10.11 | all-reduce | flops 6 | bytes 48 | tf_op jit(solution)/shard_map/psum | solution.py:158
  188.0 0.7 fusion.32
  189.2 16.5 %collective-permute-start.15 = (f32[1]{0:T(128)}, f32[1]{0:T(128)}, u32[]{:S(2)}, u32[]{:S(2)}) collective-permute-start(f32[1]{0:T(128)} %bitcast.55), channel_id=1, source_target_pairs={{16,0},{17,1},{18,2},{19,3},{20,4},{21,5},{22,6},{23,7},{24,8},{25... | collective-permute-start | bytes 20 | tf_op jit(solution)/shard_map/ppermute | solution.py:44
  206.3 1.4 dynamic-update-slice
  207.7 1.3 collective-permute-start.16
  209.0 3.8 %all-reduce = f32[2]{0:T(128)S(1)} all-reduce(f32[2]{0:T(128)S(1)} %dynamic-update-slice), channel_id=1, replica_groups=mesh['win'=2,'grp'=16] {'win'}, use_global_device_ids=true, to_apply=%add | all-reduce | flops 2 | bytes 16
  212.8 1.2 while.38
  214.2 3.1 %subtract_add_fusion.1 = (f32[2]{0:T(128)}, f32[2]{0:T(128)}) fusion(f32[2]{0:T(128)S(1)} %reduce.19, f32[2]{0:T(128)S(1)} %get-tuple-element.387, f32[]{:T(128)} %bitcast.61, f32[2]{0:T(128)S(1)} %get-tuple-element.334, f32[1]{0:T(128)} %bitcast.57, f32[1]{0:T(128)} %collective-permute-done.16, f32[1]{0:T(128)} %collective-permute-done.15, f32[1]{0:T(128)} %bitcast.54, ...), kind=kLoop, calls=%fused_computation.151 | loop fusion | flops 94 | bytes 80 | tf_op jit(solution)/shard_map/add | solution.py:168
  (169 shorter events, 18.5 us)
Async XLA Ops:
  0.6 43.5 %copy-start = (f32[4]{0:T(128)S(1)}, f32[4]{0:T(128)}, u32[]{:S(2)}) copy-start(f32[4]{0:T(128)} %param.16) | copy-start | bytes 52
  0.7 0.7 copy-start.4
  2.2 6.2 %copy-start.2 = (f32[2,6,1536]{2,0,1:T(2,128)S(1)}, f32[2,6,1536]{2,0,1:T(2,128)}, u32[]{:S(2)}) copy-start(f32[2,6,1536]{2,0,1:T(2,128)} %param.13) | copy-start | bytes 221188
  2.5 7.5 %collective-permute-start = (s32[2,1,5]{1,2,0:T(8,128)S(1)}, s32[2,1,5]{1,2,0:T(8,128)S(1)}, u32[]{:S(2)}, u32[]{:S(2)}) collective-permute-start(s32[2,1,5]{1,2,0:T(8,128)S(1)} %get-tuple-element.381), channel_id=1, source_target_pairs={{0,1},{1,0},{2,3},{3,2},{4,5},{5,4},{6,7},{7,6},{8,9},{9,8},{10,11... | collective-permute-start | bytes 128 | tf_op jit(solution)/shard_map/ppermute | solution.py:34
  4.5 7.8 %collective-permute-start.1 = (s32[2,1,5]{1,2,0:T(8,128)S(1)}, s32[2,1,5]{1,2,0:T(8,128)S(1)}, u32[]{:S(2)}, u32[]{:S(2)}) collective-permute-start(s32[2,1,5]{1,2,0:T(8,128)S(1)} %get-tuple-element.380), channel_id=1, source_target_pairs={{0,2},{1,3},{2,0},{3,1},{4,6},{5,7},{6,4},{7,5},{8,10},{9,11},{10,... | collective-permute-start | bytes 128 | tf_op jit(solution)/shard_map/ppermute | solution.py:34
  5.8 6.8 %collective-permute-start.2 = (s32[2,1,5]{1,2,0:T(8,128)S(1)}, s32[2,1,5]{1,2,0:T(8,128)S(1)}, u32[]{:S(2)}, u32[]{:S(2)}) collective-permute-start(s32[2,1,5]{1,2,0:T(8,128)S(1)} %get-tuple-element.379), channel_id=1, source_target_pairs={{0,3},{1,2},{2,1},{3,0},{4,7},{5,6},{6,5},{7,4},{8,11},{9,10},{10,... | collective-permute-start | bytes 128 | tf_op jit(solution)/shard_map/ppermute | solution.py:34
  5.8 9.3 %collective-permute-start.3 = (s32[2,1,5]{1,2,0:T(8,128)S(1)}, s32[2,1,5]{1,2,0:T(8,128)S(1)}, u32[]{:S(2)}, u32[]{:S(2)}) collective-permute-start(s32[2,1,5]{1,2,0:T(8,128)S(1)} %get-tuple-element.378), channel_id=1, source_target_pairs={{0,4},{1,5},{2,6},{3,7},{4,0},{5,1},{6,2},{7,3},{8,12},{9,13},{10,... | collective-permute-start | bytes 128 | tf_op jit(solution)/shard_map/ppermute | solution.py:34
  7.3 9.1 %collective-permute-start.4 = (s32[2,1,5]{1,2,0:T(8,128)S(1)}, s32[2,1,5]{1,2,0:T(8,128)S(1)}, u32[]{:S(2)}, u32[]{:S(2)}) collective-permute-start(s32[2,1,5]{1,2,0:T(8,128)S(1)} %get-tuple-element.377), channel_id=1, source_target_pairs={{0,5},{1,4},{2,7},{3,6},{4,1},{5,0},{6,3},{7,2},{8,13},{9,12},{10,... | collective-permute-start | bytes 128 | tf_op jit(solution)/shard_map/ppermute | solution.py:34
  9.2 0.7 copy-start.5
  9.9 9.9 %collective-permute-start.5 = (s32[2,1,5]{1,2,0:T(8,128)S(1)}, s32[2,1,5]{1,2,0:T(8,128)S(1)}, u32[]{:S(2)}, u32[]{:S(2)}) collective-permute-start(s32[2,1,5]{1,2,0:T(8,128)S(1)} %get-tuple-element.376), channel_id=1, source_target_pairs={{0,6},{1,7},{2,4},{3,5},{4,2},{5,3},{6,0},{7,1},{8,14},{9,15},{10,... | collective-permute-start | bytes 128 | tf_op jit(solution)/shard_map/ppermute | solution.py:34
  12.4 7.6 %collective-permute-start.6 = (s32[2,1,5]{1,2,0:T(8,128)S(1)}, s32[2,1,5]{1,2,0:T(8,128)S(1)}, u32[]{:S(2)}, u32[]{:S(2)}) collective-permute-start(s32[2,1,5]{1,2,0:T(8,128)S(1)} %get-tuple-element.375), channel_id=1, source_target_pairs={{0,7},{1,6},{2,5},{3,4},{4,3},{5,2},{6,1},{7,0},{8,15},{9,14},{10,... | collective-permute-start | bytes 128 | tf_op jit(solution)/shard_map/ppermute | solution.py:34
  12.6 10.9 %collective-permute-start.7 = (s32[2,1,5]{1,2,0:T(8,128)S(1)}, s32[2,1,5]{1,2,0:T(8,128)S(1)}, u32[]{:S(2)}, u32[]{:S(2)}) collective-permute-start(s32[2,1,5]{1,2,0:T(8,128)S(1)} %get-tuple-element.374), channel_id=1, source_target_pairs={{0,8},{1,9},{2,10},{3,11},{4,12},{5,13},{6,14},{7,15},{8,0},{9,1},... | collective-permute-start | bytes 128 | tf_op jit(solution)/shard_map/ppermute | solution.py:34
  15.2 9.5 %collective-permute-start.8 = (s32[2,1,5]{1,2,0:T(8,128)S(1)}, s32[2,1,5]{1,2,0:T(8,128)S(1)}, u32[]{:S(2)}, u32[]{:S(2)}) collective-permute-start(s32[2,1,5]{1,2,0:T(8,128)S(1)} %get-tuple-element.373), channel_id=1, source_target_pairs={{0,9},{1,8},{2,11},{3,10},{4,13},{5,12},{6,15},{7,14},{8,1},{9,0},... | collective-permute-start | bytes 128 | tf_op jit(solution)/shard_map/ppermute | solution.py:34
  16.3 12.7 %collective-permute-start.9 = (s32[2,1,5]{1,2,0:T(8,128)S(1)}, s32[2,1,5]{1,2,0:T(8,128)S(1)}, u32[]{:S(2)}, u32[]{:S(2)}) collective-permute-start(s32[2,1,5]{1,2,0:T(8,128)S(1)} %get-tuple-element.372), channel_id=1, source_target_pairs={{0,10},{1,11},{2,8},{3,9},{4,14},{5,15},{6,12},{7,13},{8,2},{9,3},... | collective-permute-start | bytes 128 | tf_op jit(solution)/shard_map/ppermute | solution.py:34
  19.8 9.4 %collective-permute-start.10 = (s32[2,1,5]{1,2,0:T(8,128)S(1)}, s32[2,1,5]{1,2,0:T(8,128)S(1)}, u32[]{:S(2)}, u32[]{:S(2)}) collective-permute-start(s32[2,1,5]{1,2,0:T(8,128)S(1)} %get-tuple-element.371), channel_id=1, source_target_pairs={{0,11},{1,10},{2,9},{3,8},{4,15},{5,14},{6,13},{7,12},{8,3},{9,2},... | collective-permute-start | bytes 128 | tf_op jit(solution)/shard_map/ppermute | solution.py:34
  20.0 9.3 %collective-permute-start.11 = (s32[2,1,5]{1,2,0:T(8,128)S(1)}, s32[2,1,5]{1,2,0:T(8,128)S(1)}, u32[]{:S(2)}, u32[]{:S(2)}) collective-permute-start(s32[2,1,5]{1,2,0:T(8,128)S(1)} %get-tuple-element.370), channel_id=1, source_target_pairs={{0,12},{1,13},{2,14},{3,15},{4,8},{5,9},{6,10},{7,11},{8,4},{9,5},... | collective-permute-start | bytes 128 | tf_op jit(solution)/shard_map/ppermute | solution.py:34
  23.5 6.0 %collective-permute-start.12 = (s32[2,1,5]{1,2,0:T(8,128)S(1)}, s32[2,1,5]{1,2,0:T(8,128)S(1)}, u32[]{:S(2)}, u32[]{:S(2)}) collective-permute-start(s32[2,1,5]{1,2,0:T(8,128)S(1)} %get-tuple-element.369), channel_id=1, source_target_pairs={{0,13},{1,12},{2,15},{3,14},{4,9},{5,8},{6,11},{7,10},{8,5},{9,4},... | collective-permute-start | bytes 128 | tf_op jit(solution)/shard_map/ppermute | solution.py:34
  24.6 5.3 %collective-permute-start.13 = (s32[2,1,5]{1,2,0:T(8,128)S(1)}, s32[2,1,5]{1,2,0:T(8,128)S(1)}, u32[]{:S(2)}, u32[]{:S(2)}) collective-permute-start(s32[2,1,5]{1,2,0:T(8,128)S(1)} %get-tuple-element.368), channel_id=1, source_target_pairs={{0,14},{1,15},{2,12},{3,13},{4,10},{5,11},{6,8},{7,9},{8,6},{9,7},... | collective-permute-start | bytes 128 | tf_op jit(solution)/shard_map/ppermute | solution.py:34
  29.0 6.2 %collective-permute-start.14 = (s32[2,1,5]{1,2,0:T(8,128)S(1)}, s32[2,1,5]{1,2,0:T(8,128)S(1)}, u32[]{:S(2)}, u32[]{:S(2)}) collective-permute-start(s32[2,1,5]{1,2,0:T(8,128)S(1)} %get-tuple-element.367), channel_id=1, source_target_pairs={{0,15},{1,14},{2,13},{3,12},{4,11},{5,10},{6,9},{7,8},{8,7},{9,6},... | collective-permute-start | bytes 128 | tf_op jit(solution)/shard_map/ppermute | solution.py:34
  39.3 12.9 %all-to-all-start = ((f32[2,6,16,5,128]{4,0,3,1,2:T(2,128)}), f32[2,6,16,5,128]{4,0,3,1,2:T(2,128)S(1)}, u32[]{:S(2)}, u32[]{:S(2)}) async-start(f32[2,6,16,5,128]{4,0,3,1,2:T(2,128)} %copy.137), calls=%async_computation | async-start | bytes 983040 | tf_op jit(solution)/shard_map/all_to_all | solution.py:141
  45.5 2.1 copy-start.1
  46.2 0.7 copy-start.6
  188.0 0.7 copy-start.3
  189.2 24.9 %collective-permute-start.15 = (f32[1]{0:T(128)}, f32[1]{0:T(128)}, u32[]{:S(2)}, u32[]{:S(2)}) collective-permute-start(f32[1]{0:T(128)} %bitcast.55), channel_id=1, source_target_pairs={{16,0},{17,1},{18,2},{19,3},{20,4},{21,5},{22,6},{23,7},{24,8},{25... | collective-permute-start | bytes 20 | tf_op jit(solution)/shard_map/ppermute | solution.py:44
  207.7 6.5 %collective-permute-start.16 = (f32[1]{0:T(128)}, f32[1]{0:T(128)}, u32[]{:S(2)}, u32[]{:S(2)}) collective-permute-start(f32[1]{0:T(128)} %bitcast.56), channel_id=1, source_target_pairs={{0,16},{1,17},{2,18},{3,19},{4,20},{5,21},{6,22},{7,23},{8,24},{9,... | collective-permute-start | bytes 20 | tf_op jit(solution)/shard_map/ppermute | solution.py:44
